TPU v7x, 32 devices: a whole 2x2x4 slice. The times are simulated.
32 devices in a mesh: band: 16 (over z, y, core), fft: 2 (over x).
Axes of the slice: x: 2, y: 2, z: 4, core: 2. Of those that a mesh axis runs over, the one named last changes fastest.
Arguments:
- coefficients: float32 [16, 2, 72, 5184], P('band', None, None, 'fft'), may hold values from -0.009765625 to 0.009765625
- col_index: int32 [5184], replicated, may hold values from 0 to 5183, each once
- occupation: int32 [16], P('band'), may hold values from 1 to 4
Outputs:
- density: float32 [288, 288, 288], P('band', 'fft')
Inputs may be any that keep to these rules, and one draw needn't show every extreme that they name: `col_index`: each number of the range appears once.
All inputs are finite; a program needn't handle non-finite values.
Results may differ from a plain program's by a relative error of at most 0.0003.
Values sent between devices are 32-bit elements; how exact they have to be, the bound alone decides.
A program may use at most 128 MiB of HBM per device.

v0:
```python
import math
import jax
import jax.numpy as jnp
from jax import lax
from jax.sharding import PartitionSpec as P

NC = 144
NF = 288
KZ = 72
NCOLS = 5184


def product(pattern, operand_a, operand_b):
    return jnp.einsum(pattern, operand_a, operand_b, precision=lax.Precision.HIGHEST)


def phase_tables(wave_count, offset, points):
    wave_index = jnp.arange(wave_count, dtype=jnp.int32) - offset
    grid_index = jnp.arange(points, dtype=jnp.int32)
    phases = jnp.mod(wave_index[:, None] * grid_index[None, :], points)
    angles = phases.astype(jnp.float32) * (2.0 * math.pi / points)
    return (jnp.cos(angles), jnp.sin(angles))


def interpolation_matrix(coarse_len, fine_len):
    fine_index = jnp.arange(fine_len, dtype=jnp.int32)
    coarse_index = jnp.arange(coarse_len, dtype=jnp.int32)
    wave_index = jnp.arange(1, coarse_len // 2, dtype=jnp.int32)
    offsets = fine_index[:, None] - 2 * coarse_index[None, :]
    phases = jnp.mod(offsets[:, :, None] * wave_index[None, None, :], fine_len)
    angles = phases.astype(jnp.float32) * (2.0 * math.pi / fine_len)
    return (1.0 + 2.0 * jnp.sum(jnp.cos(angles), axis=2)) / coarse_len


def rotate(pattern, real_part, imag_part, cos_table, sin_table):
    out_real = product(pattern, real_part, cos_table) - product(pattern, imag_part, sin_table)
    out_imag = product(pattern, real_part, sin_table) + product(pattern, imag_part, cos_table)
    return (out_real, out_imag)


def local(coefficients, col_index, occupation):
    band_here = coefficients.shape[0]
    col_count = coefficients.shape[3]
    band_total = band_here * lax.axis_size("band")
    radius = KZ // 2
    col_start = lax.axis_index("fft") * col_count
    local_cols = lax.dynamic_slice_in_dim(col_index, col_start, col_count)
    first_wave = local_cols // KZ - radius
    second_wave = local_cols % KZ - radius
    third_wave = jnp.arange(KZ, dtype=jnp.int32) - radius
    radial = (first_wave * first_wave + second_wave * second_wave)[None, :] + (
        third_wave * third_wave
    )[:, None]
    inside = (radial <= radius * radius).astype(jnp.float32)
    masked = coefficients * inside
    cos_table, sin_table = phase_tables(KZ, radius, NC)
    line_real, line_imag = rotate("bkc,kz->bzc", masked[:, 0], masked[:, 1], cos_table, sin_table)
    z_lines = jnp.stack([line_real, line_imag], axis=1)
    inverse = jnp.zeros((NCOLS,), jnp.int32).at[col_index].set(jnp.arange(NCOLS, dtype=jnp.int32))
    block_in = lax.all_to_all(z_lines, "fft", split_axis=2, concat_axis=3, tiled=True)
    box_grid = jnp.take(block_in, inverse, axis=3)
    box_grid = box_grid.reshape(block_in.shape[0], 2, block_in.shape[2], KZ, KZ)
    half_real, half_imag = rotate(
        "bzak,kr->bzar", box_grid[:, 0], box_grid[:, 1], cos_table, sin_table
    )
    full_real, full_imag = rotate("bzar,as->bzsr", half_real, half_imag, cos_table, sin_table)
    moduli = full_real * full_real + full_imag * full_imag
    weights = occupation.astype(jnp.float32) / band_total
    partial_value = product("b,bzxy->zxy", weights, moduli)
    interpolation = interpolation_matrix(NC, NF)
    row_share = NF // lax.axis_size("band")
    summed = lax.psum(partial_value, "band")
    own_rows = lax.dynamic_slice_in_dim(
        interpolation, lax.axis_index("band") * row_share, row_share, 0
    )
    reduced = product("zgb,fb->zgf", product("zab,ga->zgb", summed, own_rows), interpolation)
    return product(
        "rgf,hr->gfh",
        lax.all_to_all(reduced, "fft", split_axis=2, concat_axis=0, tiled=True),
        interpolation,
    )


def solution(mesh):
    return jax.shard_map(
        local,
        mesh=mesh,
        in_specs=(P("band", None, None, "fft"), P(), P("band")),
        out_specs=P("band", "fft", None),
        check_vma=False,
    )
```

profile of v0, /device:TPU:0, one launch (start us, length us, event | category | flops | bytes accessed | tf_op | source)
XLA Modules:
  0.0 451.8 jit_solution(9786847167849780601)
XLA Ops:
  6.5 0.8 fusion.105
  7.4 0.1 fusion.17
  7.5 1.6 broadcast_multiply_fusion
  9.1 1.6 fusion.18
  10.7 1.6 fusion.19
  12.4 1.7 fusion.8
  14.1 1.7 fusion.7
  15.8 0.2 pad_maximum_fusion
  16.0 0.0 copy-start.3
  16.0 3.2 copy.44
  19.3 4.2 all-to-all-start
  23.5 0.0 all-reduce.2.cloned.1.call-start
  23.5 0.0 copy-done.3
  23.5 36.3 %scatter_custom_fusion = s32[5184]{0:T(1024)S(1)} fusion(s32[5184]{0:T(1024)S(1)} %compare_select_fusion.1, s32[5184]{0:T(1024)S(1)} %iota.59, s32[]{:T(128)} %constant.53.clone.1), kind=kCustom, calls=%fused_computation.112 | custom fusion | bytes 20740 | tf_op jit(solution)/shard_map/scatter | solution.py:59
  59.8 0.1 broadcast_in_dim.27
  60.6 0.0 all-to-all-done
  60.6 6.9 %copy.62 = f32[1,2,72,2,2592]{2,1,4,3,0:T(2,128)} copy(f32[1,2,72,2,2592]{4,1,2,3,0:T(2,128)S(1)} %bitcast.89) | data formatting | bytes 5971968 | tf_op jit(solution)/shard_map/all_to_all | solution.py:60
  67.5 19.1 %gather_fusion = f32[5184,2,72]{2,1,0:T(2,128)} fusion(f32[2,72,5184]{1,0,2:T(2,128)} %bitcast.87, s32[6144]{0:T(1024)S(1)} %pad_clamp_fusion), kind=kCustom, calls=%fused_computation | custom fusion | bytes 5992704 | tf_op jit(solution)/shard_map/jit(_take)/gather | solution.py:61
  86.6 8.5 %copy.63 = f32[1,2,72,72,72]{4,3,2,1,0:T(8,128)} copy(f32[1,2,72,72,72]{2,1,4,3,0:T(2,128)} %bitcast.88) | data formatting | bytes 5971968 | tf_op jit(solution)/shard_map/jit(_take)/gather | solution.py:61
  95.0 2.9 broadcast_select_fusion
  97.9 4.8 %fusion.10 = f32[72,72,144]{2,1,0:T(8,128)S(1)} fusion(f32[1,2,72,72,72]{4,3,2,1,0:T(8,128)S(1)} %broadcast_select_fusion, s32[72]{0:T(128)S(1)} %iota_add_fusion), kind=kOutput, calls=%fused_computation.22 | convolution fusion | flops 645065856 | bytes 5640704 | tf_op jit(solution)/shard_map/bzak,kr->bzar/dot_general | solution.py:14
  102.7 4.8 %fusion.13 = f32[72,72,144]{2,1,0:T(8,128)S(1)} fusion(f32[72,72,144]{2,1,0:T(8,128)S(1)} %fusion.10, f32[1,2,72,72,72]{4,3,2,1,0:T(8,128)S(1)} %broadcast_select_fusion, s32[72]{0:T(128)S(1)} %iota_add_fusion), kind=kOutput, calls=%fused_computation.25 | convolution fusion | flops 645812352 | bytes 10949120 | tf_op jit(solution)/shard_map/bzak,kr->bzar/dot_general | solution.py:14
  107.5 11.8 %fusion.26 = f32[144,72,144]{2,0,1:T(8,128)} fusion(f32[72,72,144]{2,1,0:T(8,128)S(1)} %fusion.13, s32[72]{0:T(128)S(1)} %iota_add_fusion), kind=kOutput, calls=%fused_computation.46 | convolution fusion | flops 1290038400 | bytes 8958240 | tf_op jit(solution)/shard_map/bzar,as->bzsr/dot_general | solution.py:14
  119.3 12.0 %fusion.34 = f32[144,72,144]{2,0,1:T(8,128)} fusion(f32[72,72,144]{2,1,0:T(8,128)S(1)} %fusion.13, s32[72]{0:T(128)S(1)} %iota_add_fusion), kind=kOutput, calls=%fused_computation.54 | convolution fusion | flops 1290038400 | bytes 8958240 | tf_op jit(solution)/shard_map/bzar,as->bzsr/dot_general | solution.py:14
  131.3 4.8 %fusion.9 = f32[72,72,144]{2,1,0:T(8,128)S(1)} fusion(f32[1,2,72,72,72]{4,3,2,1,0:T(8,128)S(1)} %broadcast_select_fusion, s32[72]{0:T(128)S(1)} %iota_add_fusion), kind=kOutput, calls=%fused_computation.21 | convolution fusion | flops 645065856 | bytes 5640704 | tf_op jit(solution)/shard_map/bzak,kr->bzar/dot_general | solution.py:14
  136.1 4.8 %fusion.14 = f32[72,72,144]{2,1,0:T(8,128)S(1)} fusion(f32[72,72,144]{2,1,0:T(8,128)S(1)} %fusion.9, f32[1,2,72,72,72]{4,3,2,1,0:T(8,128)S(1)} %broadcast_select_fusion, s32[72]{0:T(128)S(1)} %iota_add_fusion), kind=kOutput, calls=%fused_computation.26 | convolution fusion | flops 645812352 | bytes 10949120 | tf_op jit(solution)/shard_map/bzak,kr->bzar/dot_general | solution.py:14
  140.9 0.0 copy-start
  140.9 11.7 %fusion.28 = f32[144,72,144]{2,0,1:T(8,128)} fusion(f32[72,72,144]{2,1,0:T(8,128)S(1)} %fusion.14, s32[72]{0:T(128)S(1)} %iota_add_fusion), kind=kOutput, calls=%fused_computation.48 | convolution fusion | flops 1290038400 | bytes 8958240 | tf_op jit(solution)/shard_map/bzar,as->bzsr/dot_general | solution.py:14
  152.6 0.0 copy-done
  152.6 21.9 %multiply_bitcast_fusion = f32[72,144,144]{2,1,0:T(8,128)} fusion(f32[144,72,144]{2,0,1:T(8,128)} %fusion.26, f32[144,72,144]{2,0,1:T(8,128)} %fusion.34, f32[144,72,144]{2,0,1:T(8,128)} %fusion.28, f32[]{:T(128)} %bitcast.1, f32[72,72,144]{2,1,0:T(8,128)} %copy-done, s32[72]{0:T(128)S(1)} %iota_add_fusion), kind=kOutput, calls=%fused_computation.11 | convolution fusion | flops 1298996352 | bytes 26874148 | tf_op jit(solution)/shard_map/bzar,as->bzsr/dot_general | solution.py:14
  174.5 0.0 all-reduce.2.cloned.1.call-update
  174.5 0.1 iota_subtract_fusion
  174.6 61.2 %fusion.3 = f32[288,144]{0,1:T(8,128)S(1)} fusion(s32[71]{0:T(128)S(1)} %iota_add_fusion.1, s32[288,144]{0,1:T(8,128)S(1)} %iota_subtract_fusion), kind=kLoop, calls=%fused_computation.6 | loop fusion | flops 29403648 | bytes 332060 | tf_op jit(solution)/shard_map/reduce_sum | solution.py:32
  235.8 0.0 copy-start.1
  235.9 144.0 %all-reduce.2.cloned.1.call-done = f32[72,144,144]{2,1,0:T(8,128)} async-done(((f32[72,144,144]{2,1,0:T(8,128)}), f32[72,144,144]{2,1,0:T(8,128)}) %all-reduce.2.cloned.1.call-update) | async-done | bytes 5971984 | tf_op jit(solution)/shard_map/psum | solution.py:72
  379.9 8.3 %convolution_bitcast_fusion = f32[72,18,144]{2,1,0:T(8,128)S(1)} fusion(f32[72,144,144]{2,1,0:T(8,128)} %all-reduce.2.cloned.1.call-done, f32[288,144]{0,1:T(8,128)S(1)} %add_multiply_fusion, s32[]{:T(128)S(6)} %select_n.74), kind=kOutput, calls=%fused_computation.27 | convolution fusion | flops 322486272 | bytes 6792196 | tf_op jit(solution)/shard_map/zab,ga->zgb/dot_general | solution.py:14
  388.2 0.0 copy-done.1
  388.2 3.8 fusion.15
  392.0 3.5 copy.54
  395.5 3.8 reshape.191
  399.2 22.0 %all_to_all.36 = f32[2,1,186624]{2,1,0:T(1,128)S(1)} all-to-all(f32[2,1,186624]{2,1,0:T(1,128)} %reshape.191), channel_id=1, replica_groups=mesh['band'=16,'fft'=2] {'fft'}, dimensions={0} | all-to-all | bytes 2985984 | tf_op jit(solution)/shard_map/all_to_all | solution.py:79
  421.2 0.6 broadcast.120
  421.8 6.2 %reduce = f32[2,186624]{1,0:T(2,128)} reduce(f32[2,1,186624]{2,1,0:T(1,128)S(1)} %all_to_all.36, f32[]{:T(128)} %broadcast.120), dimensions={1}, to_apply=%all_to_all.30.reduce_sub_computation | reduce | bytes 2985988 | tf_op jit(solution)/shard_map/all_to_all | solution.py:79
  428.0 4.1 reshape.192
  432.1 3.6 copy.72
  435.7 0.0 copy-start.2
  435.7 3.3 all_to_all.33
  439.0 0.0 copy-done.2
  439.0 5.8 %fusion.20 = f32[18,144,288]{2,1,0:T(8,128)} fusion(f32[144,18,144]{0,2,1:T(8,128)S(1)} %all_to_all.33, f32[288,144]{0,1:T(8,128)S(1)} %copy-done.2), kind=kOutput, calls=%fused_computation.37 | convolution fusion | flops 1290069504 | bytes 4644864 | tf_op jit(solution)/shard_map/rgf,hr->gfh/dot_general | solution.py:14
  (10 shorter events, 0.1 us)
Async XLA Ops:
  16.0 7.5 %copy-start.3 = (s32[5184]{0:T(1024)S(1)}, s32[5184]{0:T(1024)}, u32[]{:S(2)}) copy-start(s32[5184]{0:T(1024)} %param.4) | copy-start | bytes 62212
  19.3 41.3 %all-to-all-start = ((f32[1,2,144,2592]{3,1,0,2:T(2,128)}), f32[1,2,144,2592]{3,1,0,2:T(2,128)S(1)}, u32[]{:S(2)}, u32[]{:S(2)}) async-start(f32[1,2,144,2592]{3,1,0,2:T(2,128)} %copy.44), calls=%async_computation | async-start | bytes 6193152 | tf_op jit(solution)/shard_map/all_to_all | solution.py:60
  23.5 356.4 %all-reduce.2.cloned.1.call-start = ((), (), s32[]{:S(2)}) async-start(), calls=%async_computation.2 | async-start | bytes 21233664 | tf_op jit(solution)/shard_map/psum | solution.py:72
  140.9 11.7 %copy-start = (f32[72,72,144]{2,1,0:T(8,128)}, f32[72,72,144]{2,1,0:T(8,128)S(1)}, u32[]{:S(2)}) copy-start(f32[72,72,144]{2,1,0:T(8,128)S(1)} %fusion.14) | copy-start | bytes 8957956
  235.8 152.3 %copy-start.1 = (f32[288,144]{0,1:T(8,128)}, f32[288,144]{0,1:T(8,128)S(1)}, u32[]{:S(2)}) copy-start(f32[288,144]{0,1:T(8,128)S(1)} %fusion.3) | copy-start | bytes 497668
  435.7 3.3 copy-start.2
Sparse Core Ops, SparseCore 0:
  174.6 205.2 all-reduce.1
where the time goes:
time: 460 us; the launch traced here: 452 us
  waiting for transfers between devices  144 us (31%)
  matrix products  101 us (22%)
  local copies, waits for them, and re-layouts  92.8 us (20%)
  other arithmetic  73.2 us (16%)
  blocking collectives  22 us (5%)
  between operations  14.5 us (3%)
    psum x1, waiting for transfers between devices, local(): summed = lax.psum(partial_value, 'band')  144 us
    dot_general x15, matrix products, product(): jnp.einsum(pattern, operand_a, operand_b, precision=lax.Precision.HIGHEST)  101 us
    reduce_sum x1, other arithmetic, interpolation_matrix(): return (1.0 + 2.0 * jnp.sum(jnp.cos(angles), axis=2)) / coarse_len  61.2 us
    scatter x1, local copies, waits for them, and re-layouts, local(): jnp.zeros((NCOLS,), jnp.int32).at[col_index]  36.3 us
    gather x2, local copies, waits for them, and re-layouts, local(): box_grid = jnp.take(block_in, inverse, axis=3)  27.5 us
    all_to_all x1, blocking collectives, local(): lax.all_to_all(reduced, 'fft', split_axis=2, concat_axis=0, tiled=True)  22 us
  transfers between devices with their start and end apart: 2, of which 1 were waited for; matrix products, arithmetic and copies ran while one was open for 22% of the time, Pallas kernels for 0%

commit v1 on v0

--- a/solution.py
+++ b/solution.py
@@ -8,6 +8,14 @@
 NF = 288
 KZ = 72
 NCOLS = 5184
+
+
+def added_up(shard, name):
+    size, total = (lax.axis_size(name), shard)
+    for far in [1 << k for k in range(size.bit_length() - 1)]:
+        pairs = [(i, i ^ far) for i in range(size)]
+        total = total + lax.ppermute(total, name, pairs)
+    return total
 
 
 def product(pattern, operand_a, operand_b):
@@ -69,7 +77,7 @@
     partial_value = product("b,bzxy->zxy", weights, moduli)
     interpolation = interpolation_matrix(NC, NF)
     row_share = NF // lax.axis_size("band")
-    summed = lax.psum(partial_value, "band")
+    summed = added_up(partial_value, "band")
     own_rows = lax.dynamic_slice_in_dim(
         interpolation, lax.axis_index("band") * row_share, row_share, 0
     )

time: 460 us -> 1190 us (2.59)
  waiting for transfers between devices: 144 us -> 867 us
  between operations: 14.5 us -> 1.11 us
    ppermute x0 -> x4, waiting for transfers between devices: none -> 867 us  [added_up(): total = total + lax.ppermute(total, name, pairs)]
    psum x1 -> x0, waiting for transfers between devices: 144 us -> none  [local(): summed = lax.psum(partial_value, 'band')]
  transfers between devices with their start and end apart: 2 -> 5, of which waited for: 1 -> 4; matrix products, arithmetic and copies ran while one was open for 22% -> 8% of each run, Pallas kernels for 0% -> 0%
where the time goes in v1:
time: 1190 us; the launch traced here: 1180 us
  waiting for transfers between devices  867 us (73%)
  matrix products  103 us (9%)
  local copies, waits for them, and re-layouts  92.8 us (8%)
  other arithmetic  84.4 us (7%)
  blocking collectives  22 us (2%)
    ppermute x4, waiting for transfers between devices, added_up(): total = total + lax.ppermute(total, name, pairs)  867 us
    dot_general x15, matrix products, product(): jnp.einsum(pattern, operand_a, operand_b, precision=lax.Precision.HIGHEST)  103 us
    reduce_sum x1, other arithmetic, interpolation_matrix(): return (1.0 + 2.0 * jnp.sum(jnp.cos(angles), axis=2)) / coarse_len  61 us
    scatter x1, local copies, waits for them, and re-layouts, local(): jnp.zeros((NCOLS,), jnp.int32).at[col_index]  36.3 us
    gather x2, local copies, waits for them, and re-layouts, local(): box_grid = jnp.take(block_in, inverse, axis=3)  27.5 us
  transfers between devices with their start and end apart: 5, of which 4 were waited for; matrix products, arithmetic and copies ran while one was open for 8% of the time, Pallas kernels for 0%

profile of v1, /device:TPU:0, one launch (start us, length us, event | category | flops | bytes accessed | tf_op | source)
XLA Modules:
  0.0 1181.3 jit_solution(17955237219741524194)
XLA Ops:
  0.0 0.8 fusion.110
  0.8 0.1 fusion.22
  1.0 1.6 broadcast_multiply_fusion
  2.6 1.6 fusion.23
  4.2 1.6 fusion.24
  5.9 1.7 fusion.10
  7.6 1.7 fusion.9
  9.3 0.2 pad_maximum_fusion
  9.5 0.0 copy-start.3
  9.5 3.2 copy.44
  12.8 4.2 all-to-all-start
  17.0 0.0 copy-done.3
  17.0 36.3 %scatter_custom_fusion = s32[5184]{0:T(1024)S(1)} fusion(s32[5184]{0:T(1024)S(1)} %compare_select_fusion.1, s32[5184]{0:T(1024)S(1)} %iota.59, s32[]{:T(128)} %constant.53.clone.1), kind=kCustom, calls=%fused_computation.114 | custom fusion | bytes 20740 | tf_op jit(solution)/shard_map/scatter | solution.py:67
  53.3 0.1 broadcast_in_dim.27
  54.1 0.0 all-to-all-done
  54.1 7.0 copy.62
  61.1 19.1 %gather_fusion = f32[5184,2,72]{2,1,0:T(2,128)} fusion(f32[2,72,5184]{1,0,2:T(2,128)} %bitcast.86, s32[6144]{0:T(1024)S(1)} %pad_clamp_fusion), kind=kCustom, calls=%fused_computation | custom fusion | bytes 5992704 | tf_op jit(solution)/shard_map/jit(_take)/gather | solution.py:69
  80.1 8.5 copy.63
  88.6 2.9 broadcast_select_fusion
  91.5 4.8 fusion.12
  96.3 4.8 fusion.15
  101.1 11.8 fusion.31
  112.9 12.0 %fusion.39 = f32[144,72,144]{2,0,1:T(8,128)} fusion(f32[72,72,144]{2,1,0:T(8,128)S(1)} %fusion.15, s32[72]{0:T(128)S(1)} %iota_add_fusion), kind=kOutput, calls=%fused_computation.56 | convolution fusion | flops 1290038400 | bytes 8958240 | tf_op jit(solution)/shard_map/bzar,as->bzsr/dot_general | solution.py:22
  124.9 4.8 fusion.11
  129.7 4.8 fusion.16
  134.5 0.0 copy-start
  134.5 11.7 fusion.33
  146.2 0.0 copy-done
  146.2 21.5 %multiply_bitcast_fusion = f32[72,144,144]{2,1,0:T(8,128)} fusion(f32[144,72,144]{2,0,1:T(8,128)} %fusion.31, f32[144,72,144]{2,0,1:T(8,128)} %fusion.39, f32[144,72,144]{2,0,1:T(8,128)} %fusion.33, f32[]{:T(128)} %bitcast.1, f32[72,72,144]{2,1,0:T(8,128)} %copy-done, s32[72]{0:T(128)S(1)} %iota_add_fusion), kind=kOutput, calls=%fused_computation.11 | convolution fusion | flops 1298996352 | bytes 26874148 | tf_op jit(solution)/shard_map/bzar,as->bzsr/dot_general | solution.py:22
  167.7 0.2 collective-permute-start
  167.9 16.3 %collective-permute-done = f32[72,144,144]{2,1,0:T(8,128)S(1)} collective-permute-done((f32[72,144,144]{2,1,0:T(8,128)}, f32[72,144,144]{2,1,0:T(8,128)S(1)}, u32[]{:S(2)}, u32[]{:S(2)}) %collective-permute-start) | collective-permute-done | bytes 5972000 | tf_op jit(solution)/shard_map/ppermute | solution.py:17
  184.3 5.1 add.158
  189.4 2.8 collective-permute-start.1
  192.2 228.5 %collective-permute-done.1 = f32[72,144,144]{2,1,0:T(8,128)S(1)} collective-permute-done((f32[72,144,144]{2,1,0:T(8,128)S(1)}, f32[72,144,144]{2,1,0:T(8,128)S(1)}, u32[]{:S(2)}, u32[]{:S(2)}) %collective-permute-start.1) | collective-permute-done | bytes 5972000 | tf_op jit(solution)/shard_map/ppermute | solution.py:17
  420.7 1.4 add.159
  422.1 1.9 collective-permute-start.2
  424.0 227.9 %collective-permute-done.2 = f32[72,144,144]{2,1,0:T(8,128)S(1)} collective-permute-done((f32[72,144,144]{2,1,0:T(8,128)S(1)}, f32[72,144,144]{2,1,0:T(8,128)S(1)}, u32[]{:S(2)}, u32[]{:S(2)}) %collective-permute-start.2) | collective-permute-done | bytes 5972000 | tf_op jit(solution)/shard_map/ppermute | solution.py:17
  651.8 4.9 add.160
  656.7 2.5 collective-permute-start.3
  659.3 0.1 iota_subtract_fusion
  659.4 61.0 %fusion.3 = f32[288,144]{0,1:T(8,128)S(1)} fusion(s32[71]{0:T(128)S(1)} %iota_add_fusion.1, s32[288,144]{0,1:T(8,128)S(1)} %iota_subtract_fusion), kind=kLoop, calls=%fused_computation.6 | loop fusion | flops 29403648 | bytes 332060 | tf_op jit(solution)/shard_map/reduce_sum | solution.py:40
  720.4 0.0 copy-start.1
  720.5 393.8 %collective-permute-done.3 = f32[72,144,144]{2,1,0:T(8,128)} collective-permute-done((f32[72,144,144]{2,1,0:T(8,128)}, f32[72,144,144]{2,1,0:T(8,128)}, u32[]{:S(2)}, u32[]{:S(2)}) %collective-permute-start.3) | collective-permute-done | bytes 5972000 | tf_op jit(solution)/shard_map/ppermute | solution.py:17
  1114.3 10.2 fusion.17
  1124.5 0.0 copy-done.1
  1124.5 3.8 fusion.20
  1128.3 3.5 copy.54
  1131.8 3.8 reshape.191
  1135.6 22.0 %all_to_all.36 = f32[2,1,186624]{2,1,0:T(1,128)S(1)} all-to-all(f32[2,1,186624]{2,1,0:T(1,128)} %reshape.191), channel_id=1, replica_groups=mesh['band'=16,'fft'=2] {'fft'}, dimensions={0} | all-to-all | bytes 2985984 | tf_op jit(solution)/shard_map/all_to_all | solution.py:87
  1157.6 0.6 broadcast.120
  1158.2 6.2 reduce
  1164.3 4.1 reshape.192
  1168.4 3.6 copy.72
  1172.0 0.0 copy-start.2
  1172.0 3.3 all_to_all.33
  1175.3 0.0 copy-done.2
  1175.3 5.8 fusion.25
  (10 shorter events, 0.1 us)
Async XLA Ops:
  9.5 7.5 copy-start.3
  12.8 41.4 %all-to-all-start = ((f32[1,2,144,2592]{3,1,0,2:T(2,128)}), f32[1,2,144,2592]{3,1,0,2:T(2,128)S(1)}, u32[]{:S(2)}, u32[]{:S(2)}) async-start(f32[1,2,144,2592]{3,1,0,2:T(2,128)} %copy.44), calls=%async_computation | async-start | bytes 6193152 | tf_op jit(solution)/shard_map/all_to_all | solution.py:68
  134.5 11.7 copy-start
  167.7 16.6 %collective-permute-start = (f32[72,144,144]{2,1,0:T(8,128)}, f32[72,144,144]{2,1,0:T(8,128)S(1)}, u32[]{:S(2)}, u32[]{:S(2)}) collective-permute-start(f32[72,144,144]{2,1,0:T(8,128)} %multiply_bitcast_fusion), channel_id=1, source_target_pairs={{0,2},{2,0},{4,6},{6,4},{8,10},{10,8},{12,14},{14,12},{16,18},{18,... | collective-permute-start | bytes 17915912 | tf_op jit(solution)/shard_map/ppermute | solution.py:17
  189.4 231.3 %collective-permute-start.1 = (f32[72,144,144]{2,1,0:T(8,128)S(1)}, f32[72,144,144]{2,1,0:T(8,128)S(1)}, u32[]{:S(2)}, u32[]{:S(2)}) collective-permute-start(f32[72,144,144]{2,1,0:T(8,128)S(1)} %add.158), channel_id=1, source_target_pairs={{0,4},{2,6},{4,0},{6,2},{8,12},{10,14},{12,8},{14,10},{16,20},{18,... | collective-permute-start | bytes 17915912 | tf_op jit(solution)/shard_map/ppermute | solution.py:17
  422.1 229.7 %collective-permute-start.2 = (f32[72,144,144]{2,1,0:T(8,128)S(1)}, f32[72,144,144]{2,1,0:T(8,128)S(1)}, u32[]{:S(2)}, u32[]{:S(2)}) collective-permute-start(f32[72,144,144]{2,1,0:T(8,128)S(1)} %add.159), channel_id=1, source_target_pairs={{0,8},{2,10},{4,12},{6,14},{8,0},{10,2},{12,4},{14,6},{16,24},{18,... | collective-permute-start | bytes 17915912 | tf_op jit(solution)/shard_map/ppermute | solution.py:17
  656.7 457.5 %collective-permute-start.3 = (f32[72,144,144]{2,1,0:T(8,128)}, f32[72,144,144]{2,1,0:T(8,128)}, u32[]{:S(2)}, u32[]{:S(2)}) collective-permute-start(f32[72,144,144]{2,1,0:T(8,128)} %add.160), channel_id=1, source_target_pairs={{0,16},{2,18},{4,20},{6,22},{8,24},{10,26},{12,28},{14,30},{16,0},... | collective-permute-start | bytes 17915912 | tf_op jit(solution)/shard_map/ppermute | solution.py:17
  720.4 404.1 %copy-start.1 = (f32[288,144]{0,1:T(8,128)}, f32[288,144]{0,1:T(8,128)S(1)}, u32[]{:S(2)}) copy-start(f32[288,144]{0,1:T(8,128)S(1)} %fusion.3) | copy-start | bytes 497668
  1172.0 3.3 copy-start.2
